TPU v7x, 32 devices: a whole 2x2x4 slice. The times are simulated.
32 devices in a mesh: cell: 8 (over z, x), gene: 4 (over y, core).
Axes of the slice: x: 2, y: 2, z: 4, core: 2. Of those that a mesh axis runs over, the one named last changes fastest.
Arguments:
- counts: int32 [2048, 4096], P('cell', 'gene'), may hold values from 0 to 7
- totals: int32 [2048], P('cell'), may hold values from 1000 to 19999
- cell_factors: float32 [2048, 32], P('cell'), may hold values from -0.9 to 0.9
- gene_loadings: float32 [4096, 32], P('gene'), may hold values from -0.9 to 0.9
Outputs:
- new_factors: float32 [2048, 32], P('cell')
- new_loadings: float32 [4096, 32], P('gene')
- deviance: float32 [4096], P('gene')
All inputs are finite; a program needn't handle non-finite values.
Results may differ from a plain program's by a relative error of at most 0.0044.
Values sent between devices are 32-bit elements; how exact they have to be, the bound alone decides.
A program may use at most 128 MiB of HBM per device.

v0:
```python
import functools
import math

import jax
import jax.numpy as jnp
from jax import lax
from jax.experimental import pallas as pl
from jax.experimental.pallas import tpu as pltpu
from jax.sharding import PartitionSpec as P

RIDGE = 1.0
DAMPING = 0.1
SCALE_TOTAL = 5000.0
LANES = 128
SUB = 8
BLOCK = 256
HIGH = lax.Precision.HIGHEST
NT = (((1,), (1,)), ((), ()))
LOG2E = 1.0 / math.log(2.0)
F32 = jnp.float32
BF16 = jnp.bfloat16


def packed_rows(width):
    return sum(width - SUB * (a // SUB) for a in range(width))


def lower_table(factors):
    width = factors.shape[0]
    pieces = [factors[a : a + 1] * factors[SUB * (a // SUB) :] for a in range(width)]
    return jnp.concatenate(pieces, axis=0).astype(BF16)


def split3(x):
    first = x.astype(BF16)
    rest = x - first.astype(F32)
    second = rest.astype(BF16)
    third = (rest - second.astype(F32)).astype(BF16)
    return first, second, third


def rows_of(value, count):
    index = lax.broadcasted_iota(jnp.int32, (2 * SUB, count), 0)
    parts = [x.astype(F32) for x in value] if isinstance(value, tuple) else [value] * 3
    result = jnp.zeros((2 * SUB, count), F32)
    for place, part in enumerate(parts):
        result = jnp.where(index == place, part, result)
    return result.astype(BF16)


def fixed_side(rows, tail):
    first, second, third = (x.astype(F32) for x in split3(rows))
    stack = jnp.concatenate([first, first, second, first, third, second, tail.astype(F32)], axis=0)
    return jnp.transpose(stack).astype(BF16)


def stream_side(rows, tail):
    first, second, third = split3(rows)
    return jnp.concatenate([first, second, first, third, first, second, tail], axis=0), first


def table_of(rows, first):
    width, count = rows.shape
    ones = jnp.where(lax.broadcasted_iota(jnp.int32, (2 * SUB, count), 0) == 0, 1.0, 0.0).astype(BF16)
    return jnp.concatenate([lower_table(rows), first, ones], axis=0)


def accumulate(left, rows, tail):
    width = rows.shape[0]
    right, first = stream_side(rows, tail)
    expected = jnp.exp2(jnp.dot(left, right, preferred_element_type=F32))
    high = expected.astype(BF16)
    low = (expected - high.astype(F32)).astype(BF16)
    table = table_of(rows, first)
    sums = lax.dot_general(table, high, NT, preferred_element_type=F32)
    extra = lax.dot_general(table[packed_rows(width) :], low, NT, preferred_element_type=F32)
    return sums, extra


def solve_packed(get, right, width):
    columns, start = [], 0
    for a in range(width):
        rows = width - SUB * (a // SUB)
        columns.append(get(start, rows))
        start += rows
    diagonal = sum(columns[a][a % SUB : a % SUB + 1] for a in range(width)) / width
    shift = RIDGE + DAMPING * diagonal
    count = width // SUB
    index = lax.broadcasted_iota(jnp.int32, (width, right.shape[1]), 0)
    lower, scaled = [], []
    value = right
    for a in range(width):
        own, place = a // SUB, a % SUB
        column = columns[a]
        rows = index[: width - SUB * own]
        inverse = 1.0 / (column[place : place + 1] + shift)
        factor = jnp.where(rows > place, column * inverse, 0.0)
        for b in range(a + 1, width):
            offset = SUB * (b // SUB - own)
            coefficient = column[b - SUB * own : b - SUB * own + 1]
            columns[b] = columns[b] - factor[offset:] * coefficient
        lower.append(factor)
        head = value[SUB * own :]
        pivot = head[place : place + 1]
        scaled.append(pivot * inverse)
        head = head - factor * pivot
        value = head if own == 0 else jnp.concatenate([value[: SUB * own], head], axis=0)
    parts = [None] * count
    for a in range(width - 1, -1, -1):
        own, place = a // SUB, a % SUB
        rows = index[:SUB]
        if parts[own] is None:
            parts[own] = jnp.zeros((SUB, right.shape[1]), F32)
        known = jnp.concatenate(parts[own:], axis=0)
        found = scaled[a] - jnp.sum(lower[a] * known, axis=0, keepdims=True)
        parts[own] = jnp.where(rows == place, found, parts[own])
    return jnp.concatenate(parts, axis=0)


def solve_kernel(width, curvature_ref, gradient_ref, out_ref):
    out_ref[...] = solve_packed(
        lambda start, rows: curvature_ref[start : start + rows], gradient_ref[...], width
    )


def newton_solve(curvature, gradient):
    count, width = gradient.shape
    matrix = jnp.transpose(curvature).reshape(width, width, count)
    packed = jnp.concatenate([matrix[a, SUB * (a // SUB) :] for a in range(width)], axis=0)
    fill = -count % LANES
    packed = jnp.pad(packed, ((0, 0), (0, fill)))
    right = jnp.pad(jnp.transpose(gradient), ((0, 0), (0, fill)))
    rows = packed.shape[0]
    result = pl.pallas_call(
        functools.partial(solve_kernel, width),
        grid=((count + fill) // LANES,),
        in_specs=[
            pl.BlockSpec((rows, LANES), lambda i: (0, i)),
            pl.BlockSpec((width, LANES), lambda i: (0, i)),
        ],
        out_specs=pl.BlockSpec((width, LANES), lambda i: (0, i)),
        out_shape=jax.ShapeDtypeStruct(right.shape, F32),
    )(packed, right)
    return jnp.transpose(result[:, :count])


def outer_table(factors):
    width = factors.shape[1]
    product = factors[:, :, None] * factors[:, None, :]
    return product.reshape(factors.shape[0], width * width).astype(BF16)


def predict(offset, factors, loadings):
    linear = offset[:, None] + jnp.dot(factors, loadings.T, precision=HIGH)
    return (linear, jnp.exp(linear))


def gene_contract(counts, expected, loadings):
    weights = expected.astype(BF16)
    residual = (counts.astype(F32) - expected).astype(BF16)
    gradient = jnp.dot(residual, loadings.astype(BF16), preferred_element_type=F32)
    curvature = jnp.dot(weights, outer_table(loadings), preferred_element_type=F32)
    return (gradient, curvature)


def cell_contract(counts, linear, expected, factors):
    counts_real = counts.astype(F32)
    weights = expected.astype(BF16)
    residual = (counts_real - expected).astype(BF16)
    dims = (((0,), (0,)), ((), ()))
    gradient = lax.dot_general(residual, factors.astype(BF16), dims, preferred_element_type=F32)
    curvature = lax.dot_general(weights, outer_table(factors), dims, preferred_element_type=F32)
    terms = 2.0 * (
        counts_real * (jnp.log(jnp.maximum(counts_real, 1.0)) - linear) - counts_real + expected
    )
    return (gradient, curvature, jnp.sum(terms, axis=0))


def by_collectives(counts, totals, cell_factors, gene_loadings):
    offset = jnp.log(totals.astype(F32)) - math.log(SCALE_TOTAL)
    linear, expected = predict(offset, cell_factors, gene_loadings)
    gradient_part, curvature_part = gene_contract(counts, expected, gene_loadings)
    gradient_sum, curvature_sum = lax.psum((gradient_part, curvature_part), "gene")
    new_factors = cell_factors + newton_solve(curvature_sum, gradient_sum - RIDGE * cell_factors)
    cell_total = counts.shape[0] * lax.axis_size("cell")
    linear_next, expected_next = predict(offset, new_factors, gene_loadings)
    gradient_part, curvature_part, deviance_part = cell_contract(
        counts, linear_next, expected_next, new_factors
    )
    gradient_share, curvature_share, deviance_share = (
        lax.psum_scatter(gradient_part, "cell", scatter_dimension=0, tiled=True),
        lax.psum_scatter(curvature_part, "cell", scatter_dimension=0, tiled=True),
        lax.psum_scatter(deviance_part, "cell", scatter_dimension=0, tiled=True),
    )
    portion = gradient_share.shape[0]
    start_row = lax.axis_index("cell") * portion
    own_rows = lax.dynamic_slice_in_dim(gene_loadings, start_row, portion, 0)
    own_new = own_rows + newton_solve(curvature_share, gradient_share - RIDGE * own_rows)
    new_loadings, deviance = (
        lax.all_gather(own_new, "cell", axis=0, tiled=True),
        lax.all_gather(deviance_share / cell_total, "cell", axis=0, tiled=True),
    )
    return (new_factors, new_loadings, deviance)


def send(source, target, send_sem, recv_sem, device):
    return pltpu.make_async_remote_copy(
        src_ref=source,
        dst_ref=target,
        send_sem=send_sem,
        recv_sem=recv_sem,
        device_id=device,
        device_id_type=pl.DeviceIdType.MESH,
    )


def sweep_kernel(
    n_cell,
    n_gene,
    counts_hbm,
    totals_hbm,
    factors_hbm,
    loadings_hbm,
    new_factors_ref,
    new_loadings_ref,
    deviance_ref,
    counts_ref,
    counts_low,
    all_totals,
    factors_ref,
    loads,
    first_own,
    first_in,
    pair_own,
    pair_in,
    total,
    all_factors,
    constant_part,
    second_own,
    second_in,
    deviance_own,
    deviance_in,
    sums,
    local_sem,
    totals_out,
    totals_in,
    loads_out,
    loads_in,
    first_out_sem,
    first_in_sem,
    factors_out,
    factors_in,
    passed_out,
    passed_in,
    second_out_sem,
    second_in_sem,
    deviance_out_sem,
    deviance_in_sem,
    last_out,
    last_in,
):
    cell, gene = lax.axis_index("cell"), lax.axis_index("gene")
    width, cells = factors_ref.shape
    genes = loads.shape[2]
    half = cells // 2
    chunks = genes // BLOCK
    packed = packed_rows(width)

    def flip(index, bits, limit):
        result, bit = 0, 1
        while bit < limit:
            result = result + bit * lax.rem(lax.rem(index // bit, 2) + bits // bit % 2, 2)
            bit *= 2
        return result

    def peer(step):
        return {"cell": flip(cell, step, n_cell), "gene": gene}

    partner = {"cell": cell, "gene": flip(gene, 1, n_gene)}
    across = {"cell": cell, "gene": flip(gene, 2, n_gene)}

    barrier = pltpu.get_barrier_semaphore()
    others = [partner, across] + [peer(step) for step in range(1, n_cell)]
    for other in others:
        pl.semaphore_signal(barrier, inc=1, device_id=other, device_id_type=pl.DeviceIdType.MESH)

    local = [
        pltpu.make_async_copy(loadings_hbm, loads.at[0], local_sem.at[0]),
        pltpu.make_async_copy(totals_hbm, all_totals.at[cell], local_sem.at[1]),
        pltpu.make_async_copy(factors_hbm, factors_ref, local_sem.at[2]),
        pltpu.make_async_copy(counts_hbm, counts_ref, local_sem.at[3]),
    ]
    for copy in local:
        copy.start()

    def chunk(q):
        return pl.ds(pl.multiple_of(q * BLOCK, BLOCK), BLOCK)

    to_partner = send(loads.at[0], loads.at[1], loads_out.at[0], loads_in.at[0], partner)

    def to_across(q):
        return send(
            loads.at[0, :, chunk(q)], loads.at[2, :, chunk(q)], loads_out.at[1 + q], loads_in.at[1 + q], across
        )

    def passed_on(q):
        return send(
            loads.at[2, :, chunk(q)],
            loads.at[3, :, chunk(q)],
            loads_out.at[1 + chunks + q],
            loads_in.at[1 + chunks + q],
            partner,
        )

    def totals_copy(step):
        return send(
            all_totals.at[cell], all_totals.at[cell], totals_out.at[step], totals_in.at[step], peer(step)
        )

    first_copy = send(first_own, first_in, first_out_sem.at[0], first_in_sem.at[0], partner)
    pair_copy = send(pair_own, pair_in, first_out_sem.at[1], first_in_sem.at[1], across)

    local[0].wait()
    local[1].wait()
    with jax.named_scope("z_barrier"):
        pl.semaphore_wait(barrier, len(others))
    for q in range(chunks):
        to_across(q).start()
    to_partner.start()
    for step in range(n_cell - 1, 0, -1):
        totals_copy(step).start()

    local[2].wait()
    offset = jnp.log(all_totals[cell].astype(F32)) - math.log(SCALE_TOTAL)
    with jax.named_scope("a_left"):
        left = fixed_side(factors_ref[...] * LOG2E, rows_of(split3(offset * LOG2E), cells))
    total[...] = jnp.zeros_like(total)
    first_own[...] = jnp.zeros_like(first_own)
    ones = rows_of(1.0, BLOCK)

    def add_genes(slot, q):
        part, extra = accumulate(left, loads[slot, :, chunk(q)], ones)
        total[...] += part
        total[packed:] += extra

    with jax.named_scope("b_countswait"):
        local[3].wait()

    with jax.named_scope("c_counts"):

        @pl.loop(0, chunks)
        def _(q):
            where = chunk(q)
            real = counts_ref[:, where].astype(F32)
            low = real.astype(BF16)
            counts_low[:, where] = low
            constant_part[:, where] = jnp.sum(
                real * jnp.log(jnp.maximum(real, 1.0)) - real, axis=0, keepdims=True
            )
            first_own[...] += lax.dot_general(
                loads[0, :, where].astype(BF16), low, NT, preferred_element_type=F32
            )

    first_copy.start()

    with jax.named_scope("d_own"):

        @pl.loop(0, chunks)
        def _(q):
            add_genes(0, q)

    with jax.named_scope("e_first"):
        first_copy.wait_recv()
        pair_own[...] = first_own[...] + first_in[...]
        pair_copy.start()
        to_partner.wait_recv()

    with jax.named_scope("f_partner"):

        @pl.loop(0, chunks)
        def _(q):
            add_genes(1, q)

    with jax.named_scope("g_wait0"):
        to_across(0).wait_recv()
        passed_on(0).start()
    add_genes(2, 0)

    @pl.loop(1, chunks)
    def _(q):
        with jax.named_scope("g_wait1"):
            to_across(q).wait_recv()
            passed_on(q).start()
        with jax.named_scope("g_add1"):
            add_genes(2, q)
        with jax.named_scope("g_wait2"):
            passed_on(q - 1).wait_recv()
        with jax.named_scope("g_add2"):
            add_genes(3, q - 1)

    with jax.named_scope("g_wait3"):
        passed_on(chunks - 1).wait_recv()
    add_genes(3, chunks - 1)
    with jax.named_scope("g_wait4"):
        pair_copy.wait_recv()

    with jax.named_scope("h_solve1"):
        old = factors_ref[...]
        counted = pair_own[...] + pair_in[...]
        gradient = counted - total[packed : packed + width] - RIDGE * old
        found = old + solve_packed(lambda start, rows: total[start : start + rows], gradient, width)
        new_factors_ref[...] = found
        all_factors[cell] = found

    mine = pl.ds(pl.multiple_of(lax.rem(gene, 2) * half, half), half)
    theirs = pl.ds(pl.multiple_of(half - lax.rem(gene, 2) * half, half), half)

    def factors_copy(step):
        return send(
            new_factors_ref.at[:, mine],
            all_factors.at[cell, :, mine],
            factors_out.at[step],
            factors_in.at[step],
            peer(step),
        )

    def factors_pass(step):
        place = all_factors.at[flip(cell, step, n_cell), :, mine]
        return send(place, place, passed_out.at[step], passed_in.at[step], partner)

    for step in range(n_cell - 1, 0, -1):
        factors_copy(step).start()

    with jax.named_scope("i_second"):
        first, second, _ = split3(new_factors_ref[...])
        stack = jnp.concatenate([first, second, rows_of(split3(offset), cells)], axis=0)

        @pl.loop(0, chunks)
        def _(q):
            where = chunk(q)
            part = jnp.dot(stack, counts_low[:, where], preferred_element_type=F32)
            second_own[:, where] = part[:width]
            whole = loads[0, :, where] * (part[:width] + part[width : 2 * width])
            known = jnp.sum(whole, axis=0, keepdims=True)
            for row in range(3):
                known = known + part[2 * width + row : 2 * width + row + 1]
            deviance_own[:, where] = 2.0 * (constant_part[:, where] - known)

    def lanes(index):
        return pl.ds(pl.multiple_of(index * LANES, LANES), LANES)

    def second_copy(step):
        return send(
            second_own.at[:, lanes(flip(cell, step, n_cell))],
            second_in.at[cell],
            second_out_sem.at[step],
            second_in_sem.at[step],
            peer(step),
        )

    def deviance_copy(step):
        return send(
            deviance_own.at[:, lanes(flip(cell, step, n_cell))],
            deviance_in.at[cell],
            deviance_out_sem.at[step],
            deviance_in_sem.at[step],
            peer(step),
        )

    for step in range(n_cell - 1, 0, -1):
        second_copy(step).start()
        deviance_copy(step).start()

    with jax.named_scope("j_left"):
        own_rows = loads[0, :, lanes(cell)]
        left = fixed_side(own_rows * LOG2E, rows_of(1.0, LANES))
    sums[...] = jnp.zeros_like(sums)

    def add_cells(index):
        offsets = jnp.log(all_totals[index].astype(F32)) - math.log(SCALE_TOTAL)
        part, extra = accumulate(left, all_factors[index], rows_of(split3(offsets * LOG2E), cells))
        sums[...] += part
        sums[packed:] += extra

    with jax.named_scope("k_own"):
        add_cells(cell)

    def take(step):
        totals_copy(step).wait_recv()
        factors_copy(step).wait_recv()
        factors_pass(step).start()

    def passed_to(step):
        place = all_factors.at[flip(cell, step, n_cell), :, theirs]
        return send(place, place, passed_out.at[step], passed_in.at[step], partner)

    with jax.named_scope("l_wait0"):
        take(1)

    for step in range(2, n_cell):
        with jax.named_scope("l_wait1"):
            take(step)
        with jax.named_scope("l_wait2"):
            passed_to(step - 1).wait_recv()
        with jax.named_scope("l_add"):
            add_cells(flip(cell, step - 1, n_cell))
    with jax.named_scope("l_wait3"):
        passed_to(n_cell - 1).wait_recv()
    with jax.named_scope("l_add"):
        add_cells(flip(cell, n_cell - 1, n_cell))

    with jax.named_scope("m_wait"):
        for step in range(1, n_cell):
            second_copy(step).wait_recv()
            deviance_copy(step).wait_recv()

    with jax.named_scope("n_solve2"):
        counted = second_own[:, lanes(cell)]
        deviance = deviance_own[:, lanes(cell)]
        for step in range(1, n_cell):
            counted = counted + second_in[flip(cell, step, n_cell)]
            deviance = deviance + deviance_in[flip(cell, step, n_cell)]
        gradient = counted - sums[packed : packed + width] - RIDGE * own_rows
        new_rows = own_rows + solve_packed(lambda start, rows: sums[start : start + rows], gradient, width)
        plain = sums[packed + width : packed + width + 1]
        new_loadings_ref[:, lanes(cell)] = new_rows
        deviance_ref[:, lanes(cell)] = (deviance + 2.0 * plain) / (cells * n_cell)

    def last_copy(step, which):
        ref = (new_loadings_ref, deviance_ref)[which]
        place = ref.at[:, lanes(cell)]
        return send(place, place, last_out.at[which, step], last_in.at[which, step], peer(step))

    for step in range(n_cell - 1, 0, -1):
        last_copy(step, 0).start()
        last_copy(step, 1).start()
    with jax.named_scope("o_sends"):
        to_partner.wait_send()
        first_copy.wait_send()
        pair_copy.wait_send()
        for q in range(chunks):
            to_across(q).wait_send()
            passed_on(q).wait_send()
        for step in range(1, n_cell):
            totals_copy(step).wait_send()
            factors_copy(step).wait_send()
            factors_pass(step).wait_send()
            second_copy(step).wait_send()
            deviance_copy(step).wait_send()
    with jax.named_scope("p_last"):
        for step in range(1, n_cell):
            last_copy(step, 0).wait_send()
            last_copy(step, 1).wait_send()
        for step in range(1, n_cell):
            last_copy(step, 0).wait_recv()
            last_copy(step, 1).wait_recv()


def finish_kernel(*refs):
    count = len(refs) // 2
    sem = refs[-1]
    copies = [pltpu.make_async_copy(refs[i], refs[count + i], sem.at[i]) for i in range(count)]
    for copy in copies:
        copy.start()
    for copy in copies:
        copy.wait()


def by_kernel(n_cell, n_gene, counts, totals, cell_factors, gene_loadings):
    cells, genes = counts.shape
    width = cell_factors.shape[1]
    rows = packed_rows(width) + width + 2 * SUB
    chunks = genes // BLOCK
    vmem = pl.BlockSpec(memory_space=pltpu.VMEM)
    hbm = pl.BlockSpec(memory_space=pltpu.HBM)
    dma = lambda *n: pltpu.SemaphoreType.DMA(n)
    shapes = (
        jax.ShapeDtypeStruct((width, cells), F32),
        jax.ShapeDtypeStruct((width, genes), F32),
        jax.ShapeDtypeStruct((1, genes), F32),
    )
    results = pl.pallas_call(
        functools.partial(sweep_kernel, n_cell, n_gene),
        out_shape=shapes,
        in_specs=[hbm] * 4,
        out_specs=(vmem,) * 3,
        scratch_shapes=[
            pltpu.VMEM((cells, genes), jnp.int32),
            pltpu.VMEM((cells, genes), BF16),
            pltpu.VMEM((n_cell, 1, cells), jnp.int32),
            pltpu.VMEM((width, cells), F32),
            pltpu.VMEM((n_gene, width, genes), F32),
            pltpu.VMEM((width, cells), F32),
            pltpu.VMEM((width, cells), F32),
            pltpu.VMEM((width, cells), F32),
            pltpu.VMEM((width, cells), F32),
            pltpu.VMEM((rows, cells), F32),
            pltpu.VMEM((n_cell, width, cells), F32),
            pltpu.VMEM((1, genes), F32),
            pltpu.VMEM((width, genes), F32),
            pltpu.VMEM((n_cell, width, LANES), F32),
            pltpu.VMEM((1, genes), F32),
            pltpu.VMEM((n_cell, 1, LANES), F32),
            pltpu.VMEM((rows, LANES), F32),
            dma(4),
            dma(n_cell),
            dma(n_cell),
            dma(1 + 2 * chunks),
            dma(1 + 2 * chunks),
            dma(2),
            dma(2),
            dma(n_cell),
            dma(n_cell),
            dma(n_cell),
            dma(n_cell),
            dma(n_cell),
            dma(n_cell),
            dma(n_cell),
            dma(n_cell),
            dma(2, n_cell),
            dma(2, n_cell),
        ],
        compiler_params=pltpu.CompilerParams(
            collective_id=0, has_side_effects=True, vmem_limit_bytes=24000 * 1024
        ),
    )(counts, totals.reshape(1, cells), cell_factors.T, gene_loadings.T)
    new_factors, new_loadings, deviance = pl.pallas_call(
        finish_kernel,
        out_shape=shapes,
        in_specs=[vmem] * 3,
        out_specs=(hbm,) * 3,
        scratch_shapes=[dma(3)],
        compiler_params=pltpu.CompilerParams(vmem_limit_bytes=8000 * 1024),
    )(*results)
    return (new_factors.T, new_loadings.T, deviance.reshape(genes))


def solution(mesh):
    n_cell, n_gene = mesh.shape["cell"], mesh.shape["gene"]

    def on_device(counts, totals, cell_factors, gene_loadings):
        cells, genes = counts.shape
        whole_lanes = genes == n_cell * LANES and cells == 2 * LANES and genes % BLOCK == 0
        if whole_lanes and n_gene == 4 and n_cell & (n_cell - 1) == 0:
            return by_kernel(n_cell, n_gene, counts, totals, cell_factors, gene_loadings)
        return by_collectives(counts, totals, cell_factors, gene_loadings)

    return jax.shard_map(
        on_device,
        mesh=mesh,
        in_specs=(P("cell", "gene"), P("cell"), P("cell", None), P("gene", None)),
        out_specs=(P("cell", None), P("gene", None), P("gene")),
        check_vma=False,
    )
```

profile of v0, /device:TPU:0, one launch (start us, length us, event | category | flops | bytes accessed | tf_op | source)
XLA Modules:
  0.0 37.2 jit_solution(8055419750952192500)
XLA Ops:
  0.6 0.0 copy-start.3
  0.6 0.7 %copy-done.3 = s32[256]{0:T(256)S(1)} copy-done((s32[256]{0:T(256)S(1)}, s32[256]{0:T(256)}, u32[]{:S(2)}) %copy-start.3) | copy-done | bytes 1048
  1.3 0.0 copy-start
  1.3 1.2 %copy-done = s32[256,1024]{1,0:T(8,128)S(1)} copy-done((s32[256,1024]{1,0:T(8,128)S(1)}, s32[256,1024]{1,0:T(8,128)}, u32[]{:S(2)}) %copy-start) | copy-done | bytes 1048600
  2.5 0.0 copy-start.1
  2.5 0.9 %copy-done.1 = f32[1024,32]{0,1:T(8,128)S(1)} copy-done((f32[1024,32]{0,1:T(8,128)S(1)}, f32[1024,32]{0,1:T(8,128)}, u32[]{:S(2)}) %copy-start.1) | copy-done | bytes 131096
  3.4 0.0 copy-start.2
  3.4 0.8 %copy-done.2 = f32[256,32]{0,1:T(8,128)S(1)} copy-done((f32[256,32]{0,1:T(8,128)S(1)}, f32[256,32]{0,1:T(8,128)}, u32[]{:S(2)}) %copy-start.2) | copy-done | bytes 32792
  4.2 32.3 %shard_map.67 = (f32[32,256]{1,0:T(8,128)S(1)}, f32[32,1024]{1,0:T(8,128)S(1)}, f32[1,1024]{1,0:T(1,128)S(1)}) custom-call(s32[256,1024]{1,0:T(8,128)S(1)} %copy-done, s32[1,256]{1,0:T(1,128)S(1)} %bitcast.8, f32[32,256]{1,0:T(8,128)S(1)} %bitcast.7, f32[32,1024]{1,0:T(8,128)S(1)} %bitcast.6), custom_call_target="tpu_custom_call" | custom-call | tf_op jit(solution)/shard_map/pallas_call | solution.py:582
  36.5 0.7 %shard_map.68 = (f32[32,256]{1,0:T(8,128)}, f32[32,1024]{1,0:T(8,128)}, f32[1,1024]{1,0:T(1,128)}) custom-call(f32[32,256]{1,0:T(8,128)S(1)} %get-tuple-element.9.refs_0_, f32[32,1024]{1,0:T(8,128)S(1)} %get-tuple-element.10.refs_1_, f32[1,1024]{1,0:T(1,128)S(1)} %get-tuple-element.11.refs_2_), custom_call_target="tpu_custom_call" | custom-call | tf_op jit(solution)/shard_map/pallas_call | solution.py:627
Async XLA Ops:
  0.6 0.7 %copy-start.3 = (s32[256]{0:T(256)S(1)}, s32[256]{0:T(256)}, u32[]{:S(2)}) copy-start(s32[256]{0:T(256)} %param.5) | copy-start | bytes 3076
  1.3 1.2 %copy-start = (s32[256,1024]{1,0:T(8,128)S(1)}, s32[256,1024]{1,0:T(8,128)}, u32[]{:S(2)}) copy-start(s32[256,1024]{1,0:T(8,128)} %counts_hbm.1) | copy-start | bytes 3145732
  2.5 0.9 %copy-start.1 = (f32[1024,32]{0,1:T(8,128)S(1)}, f32[1024,32]{0,1:T(8,128)}, u32[]{:S(2)}) copy-start(f32[1024,32]{0,1:T(8,128)} %param.7) | copy-start | bytes 393220
  3.4 0.8 %copy-start.2 = (f32[256,32]{0,1:T(8,128)S(1)}, f32[256,32]{0,1:T(8,128)}, u32[]{:S(2)}) copy-start(f32[256,32]{0,1:T(8,128)} %param.6) | copy-start | bytes 98308
where the time goes:
time: 37.4 us; the launch traced here: 37.2 us
  Pallas kernels  33 us (88%)
  local copies, waits for them, and re-layouts  3.56 us (10%)
  between operations  0.65 us (2%)
    pallas_call x1, Pallas kernels, by_kernel(): pl.pallas_call(functools.partial(sweep_kernel, n_cell, n_gene), out_shape...  32.3 us
    unnamed x8, local copies, waits for them, and re-layouts  3.56 us

commit v1 on v0

v1 whole, which is shorter than its diff:
```python
import functools
import math

import jax
import jax.numpy as jnp
from jax import lax
from jax.experimental import pallas as pl
from jax.experimental.pallas import tpu as pltpu
from jax.sharding import PartitionSpec as P

RIDGE = 1.0
DAMPING = 0.1
SCALE_TOTAL = 5000.0
LANES = 128
SUB = 8
BLOCK = 256
HIGH = lax.Precision.HIGHEST
NT = (((1,), (1,)), ((), ()))
LOG2E = 1.0 / math.log(2.0)
F32 = jnp.float32
BF16 = jnp.bfloat16


def packed_rows(width):
    return sum(width - SUB * (a // SUB) for a in range(width))


def lower_table(factors):
    width = factors.shape[0]
    pieces = [factors[a : a + 1] * factors[SUB * (a // SUB) :] for a in range(width)]
    return jnp.concatenate(pieces, axis=0).astype(BF16)


def split3(x):
    first = x.astype(BF16)
    rest = x - first.astype(F32)
    second = rest.astype(BF16)
    third = (rest - second.astype(F32)).astype(BF16)
    return first, second, third


def rows_of(value, count):
    index = lax.broadcasted_iota(jnp.int32, (2 * SUB, count), 0)
    parts = [x.astype(F32) for x in value] if isinstance(value, tuple) else [value] * 3
    result = jnp.zeros((2 * SUB, count), F32)
    for place, part in enumerate(parts):
        result = jnp.where(index == place, part, result)
    return result.astype(BF16)


def fixed_side(rows, tail):
    first, second, third = (x.astype(F32) for x in split3(rows))
    stack = jnp.concatenate([first, first, second, first, third, second, tail.astype(F32)], axis=0)
    return jnp.transpose(stack).astype(BF16)


def stream_side(rows, tail):
    first, second, third = split3(rows)
    return jnp.concatenate([first, second, first, third, first, second, tail], axis=0), first


def table_of(rows, first):
    width, count = rows.shape
    ones = jnp.where(lax.broadcasted_iota(jnp.int32, (2 * SUB, count), 0) == 0, 1.0, 0.0).astype(BF16)
    return jnp.concatenate([lower_table(rows), first, ones], axis=0)


def accumulate(left, rows, tail):
    width = rows.shape[0]
    right, first = stream_side(rows, tail)
    expected = jnp.exp2(jnp.dot(left, right, preferred_element_type=F32))
    high = expected.astype(BF16)
    low = (expected - high.astype(F32)).astype(BF16)
    table = table_of(rows, first)
    sums = lax.dot_general(table, high, NT, preferred_element_type=F32)
    extra = lax.dot_general(table[packed_rows(width) :], low, NT, preferred_element_type=F32)
    return sums, extra


def solve_packed(get, right, width, lower_ref):
    columns, start = [], 0
    groups = right.shape[1] // LANES
    for a in range(width):
        rows = width - SUB * (a // SUB)
        columns.append(get(start, rows))
        start += rows
    diagonal = sum(columns[a][a % SUB : a % SUB + 1] for a in range(width)) / width
    shift = RIDGE + DAMPING * diagonal
    count = width // SUB
    index = lax.broadcasted_iota(jnp.int32, (width, right.shape[1]), 0)
    scaled = []
    value = right
    for a in range(width):
        own, place = a // SUB, a % SUB
        column = columns[a]
        rows = index[: width - SUB * own]
        inverse = 1.0 / (column[place : place + 1] + shift)
        factor = jnp.where(rows > place, column * inverse, 0.0)
        for b in range(a + 1, width):
            offset = SUB * (b // SUB - own)
            coefficient = column[b - SUB * own : b - SUB * own + 1]
            columns[b] = columns[b] - factor[offset:] * coefficient
        for group in range(groups):
            lower_ref[group, width * a + SUB * own : width * (a + 1)] = factor[
                :, group * LANES : (group + 1) * LANES
            ]
        head = value[SUB * own :]
        pivot = head[place : place + 1]
        scaled.append(pivot * inverse)
        head = head - factor * pivot
        value = head if own == 0 else jnp.concatenate([value[: SUB * own], head], axis=0)
    stripe = index[:SUB]
    parts = []
    for block in range(count):
        part = jnp.zeros((SUB, right.shape[1]), F32)
        for place in range(SUB):
            part = jnp.where(stripe == place, scaled[SUB * block + place], part)
        parts.append(part)
    for a in range(width - 1, 0, -1):
        own, place = a // SUB, a % SUB
        found = parts[own][place : place + 1]
        for block in range(own + (place > 0)):
            rows = pl.ds(SUB * block * width + a, SUB, stride=width)
            row = jnp.concatenate([lower_ref[group, rows, :] for group in range(groups)], axis=1)
            parts[block] = parts[block] - row * found
    return jnp.concatenate(parts, axis=0)


def solve_kernel(width, curvature_ref, gradient_ref, out_ref, lower_ref):
    out_ref[...] = solve_packed(
        lambda start, rows: curvature_ref[start : start + rows], gradient_ref[...], width, lower_ref
    )


def newton_solve(curvature, gradient):
    count, width = gradient.shape
    matrix = jnp.transpose(curvature).reshape(width, width, count)
    packed = jnp.concatenate([matrix[a, SUB * (a // SUB) :] for a in range(width)], axis=0)
    fill = -count % LANES
    packed = jnp.pad(packed, ((0, 0), (0, fill)))
    right = jnp.pad(jnp.transpose(gradient), ((0, 0), (0, fill)))
    rows = packed.shape[0]
    result = pl.pallas_call(
        functools.partial(solve_kernel, width),
        grid=((count + fill) // LANES,),
        in_specs=[
            pl.BlockSpec((rows, LANES), lambda i: (0, i)),
            pl.BlockSpec((width, LANES), lambda i: (0, i)),
        ],
        out_specs=pl.BlockSpec((width, LANES), lambda i: (0, i)),
        out_shape=jax.ShapeDtypeStruct(right.shape, F32),
        scratch_shapes=[pltpu.VMEM((1, width * width, LANES), F32)],
    )(packed, right)
    return jnp.transpose(result[:, :count])


def outer_table(factors):
    width = factors.shape[1]
    product = factors[:, :, None] * factors[:, None, :]
    return product.reshape(factors.shape[0], width * width).astype(BF16)


def predict(offset, factors, loadings):
    linear = offset[:, None] + jnp.dot(factors, loadings.T, precision=HIGH)
    return (linear, jnp.exp(linear))


def gene_contract(counts, expected, loadings):
    weights = expected.astype(BF16)
    residual = (counts.astype(F32) - expected).astype(BF16)
    gradient = jnp.dot(residual, loadings.astype(BF16), preferred_element_type=F32)
    curvature = jnp.dot(weights, outer_table(loadings), preferred_element_type=F32)
    return (gradient, curvature)


def cell_contract(counts, linear, expected, factors):
    counts_real = counts.astype(F32)
    weights = expected.astype(BF16)
    residual = (counts_real - expected).astype(BF16)
    dims = (((0,), (0,)), ((), ()))
    gradient = lax.dot_general(residual, factors.astype(BF16), dims, preferred_element_type=F32)
    curvature = lax.dot_general(weights, outer_table(factors), dims, preferred_element_type=F32)
    terms = 2.0 * (
        counts_real * (jnp.log(jnp.maximum(counts_real, 1.0)) - linear) - counts_real + expected
    )
    return (gradient, curvature, jnp.sum(terms, axis=0))


def by_collectives(counts, totals, cell_factors, gene_loadings):
    offset = jnp.log(totals.astype(F32)) - math.log(SCALE_TOTAL)
    linear, expected = predict(offset, cell_factors, gene_loadings)
    gradient_part, curvature_part = gene_contract(counts, expected, gene_loadings)
    gradient_sum, curvature_sum = lax.psum((gradient_part, curvature_part), "gene")
    new_factors = cell_factors + newton_solve(curvature_sum, gradient_sum - RIDGE * cell_factors)
    cell_total = counts.shape[0] * lax.axis_size("cell")
    linear_next, expected_next = predict(offset, new_factors, gene_loadings)
    gradient_part, curvature_part, deviance_part = cell_contract(
        counts, linear_next, expected_next, new_factors
    )
    gradient_share, curvature_share, deviance_share = (
        lax.psum_scatter(gradient_part, "cell", scatter_dimension=0, tiled=True),
        lax.psum_scatter(curvature_part, "cell", scatter_dimension=0, tiled=True),
        lax.psum_scatter(deviance_part, "cell", scatter_dimension=0, tiled=True),
    )
    portion = gradient_share.shape[0]
    start_row = lax.axis_index("cell") * portion
    own_rows = lax.dynamic_slice_in_dim(gene_loadings, start_row, portion, 0)
    own_new = own_rows + newton_solve(curvature_share, gradient_share - RIDGE * own_rows)
    new_loadings, deviance = (
        lax.all_gather(own_new, "cell", axis=0, tiled=True),
        lax.all_gather(deviance_share / cell_total, "cell", axis=0, tiled=True),
    )
    return (new_factors, new_loadings, deviance)


def send(source, target, send_sem, recv_sem, device):
    return pltpu.make_async_remote_copy(
        src_ref=source,
        dst_ref=target,
        send_sem=send_sem,
        recv_sem=recv_sem,
        device_id=device,
        device_id_type=pl.DeviceIdType.MESH,
    )


def sweep_kernel(
    n_cell,
    n_gene,
    counts_hbm,
    totals_hbm,
    factors_hbm,
    loadings_hbm,
    new_factors_ref,
    new_loadings_ref,
    deviance_ref,
    counts_ref,
    counts_low,
    all_totals,
    factors_ref,
    loads,
    first_own,
    first_in,
    pair_own,
    pair_in,
    total,
    all_factors,
    constant_part,
    second_own,
    second_in,
    deviance_own,
    deviance_in,
    sums,
    lower_ref,
    local_sem,
    send_sem,
    once_in,
    loads_in,
    factors_in,
    relay_in,
    passed_in,
):
    cell, gene = lax.axis_index("cell"), lax.axis_index("gene")
    width, cells = factors_ref.shape
    genes = loads.shape[2]
    half = cells // 2
    chunks = genes // BLOCK
    packed = packed_rows(width)

    def flip(index, bits, limit):
        result, bit = 0, 1
        while bit < limit:
            result = result + bit * lax.rem(lax.rem(index // bit, 2) + bits // bit % 2, 2)
            bit *= 2
        return result

    def near(step):
        return flip(cell, step, n_cell)

    def peer(step):
        return {"cell": near(step), "gene": gene}

    def lanes(index):
        return pl.ds(pl.multiple_of(index * LANES, LANES), LANES)

    def chunk(q):
        return slice(q * BLOCK, (q + 1) * BLOCK)

    def take_all(view, sem):
        pltpu.make_async_copy(view, view, sem).wait()

    partner = {"cell": cell, "gene": flip(gene, 1, n_gene)}
    across = {"cell": cell, "gene": flip(gene, 2, n_gene)}
    core = lax.rem(gene, 2)
    mine, theirs = lanes(core), lanes(1 - core)
    out_totals, out_across, out_partner, out_passed, out_first, out_pair = (send_sem.at[k] for k in range(6))
    out_own, out_factors, out_relay, out_turn, out_second, out_deviance = (send_sem.at[k] for k in range(6, 12))
    out_last, out_tail = (send_sem.at[k] for k in range(12, 14))
    in_totals, in_first, in_pair, in_own = (once_in.at[k] for k in range(4))
    in_second, in_deviance, in_last, in_tail = (once_in.at[k] for k in range(4, 8))
    steps = list(range(n_cell - 1, 0, -1))
    far = [step for step in steps if step % 2 == 0]

    barrier = pltpu.get_barrier_semaphore()
    others = [partner, across] + [peer(step) for step in steps]
    for other in others:
        pl.semaphore_signal(barrier, inc=1, device_id=other, device_id_type=pl.DeviceIdType.MESH)

    local = [
        pltpu.make_async_copy(loadings_hbm, loads.at[0], local_sem.at[0]),
        pltpu.make_async_copy(totals_hbm, all_totals.at[cell], local_sem.at[1]),
        pltpu.make_async_copy(factors_hbm, factors_ref, local_sem.at[2]),
        pltpu.make_async_copy(counts_hbm, counts_ref, local_sem.at[3]),
    ]
    for copy in local:
        copy.start()

    to_partner = send(loads.at[0], loads.at[1], out_partner, loads_in.at[0], partner)

    def to_across(q):
        return send(loads.at[0, :, chunk(q)], loads.at[2, :, chunk(q)], out_across, loads_in.at[1 + q], across)

    def passed_on(q):
        where = chunk(q)
        return send(loads.at[2, :, where], loads.at[3, :, where], out_passed, loads_in.at[1 + chunks + q], partner)

    local[0].wait()
    local[1].wait()
    with jax.named_scope("z_barrier"):
        pl.semaphore_wait(barrier, len(others))
    for q in range(chunks):
        to_across(q).start()
    to_partner.start()
    for step in steps:
        send(all_totals.at[cell], all_totals.at[cell], out_totals, in_totals, peer(step)).start()

    local[2].wait()
    offset = jnp.log(all_totals[cell].astype(F32)) - math.log(SCALE_TOTAL)
    own_offset = jnp.log(all_totals[cell, :, mine].astype(F32)) - math.log(SCALE_TOTAL)
    old = factors_ref[:, mine]
    with jax.named_scope("a_left"):
        left = fixed_side(old * LOG2E, rows_of(split3(own_offset * LOG2E), LANES))

    def add_genes(slot, begin, count):
        part, extra = accumulate(left, loads[slot, :, begin : begin + count], rows_of(1.0, count))
        total[...] += part
        total[packed:] += extra

    with jax.named_scope("b_own"):
        part, extra = accumulate(left, loads[0], rows_of(1.0, genes))
        total[...] = part
        total[packed:] += extra

    with jax.named_scope("c_counts"):
        local[3].wait()
        real = counts_ref[...].astype(F32)
        low = real.astype(BF16)
        counts_low[...] = low
        constant_part[...] = jnp.sum(real * jnp.log(jnp.maximum(real, 1.0)) - real, axis=0, keepdims=True)
        first_own[...] = lax.dot_general(loads[0].astype(BF16), low, NT, preferred_element_type=F32)
    first_copy = send(first_own.at[:, theirs], first_in, out_first, in_first, partner)
    first_copy.start()
    own_rows = loads[0, :, lanes(cell)]
    second_left = fixed_side(own_rows * LOG2E, rows_of(1.0, LANES))

    with jax.named_scope("e_first"):
        to_partner.wait_recv()
    with jax.named_scope("f_partner"):
        add_genes(1, 0, genes)
        first_copy.wait_recv()
        pair_own[...] = first_own[:, mine] + first_in[...]
        pair_copy = send(pair_own, pair_in, out_pair, in_pair, across)
        pair_copy.start()

    def arrive(q):
        with jax.named_scope("g_wait_y"):
            to_across(q).wait_recv()
            passed_on(q).start()

    def arrive_passed(q):
        with jax.named_scope("g_wait_p"):
            passed_on(q).wait_recv()

    arrive(0)
    arrive(1)
    with jax.named_scope("g_add"):
        add_genes(2, 0, 2 * BLOCK)
    arrive(2)
    arrive_passed(0)
    arrive_passed(1)
    with jax.named_scope("g_add"):
        add_genes(3, 0, 2 * BLOCK)
    arrive(3)
    with jax.named_scope("g_add"):
        add_genes(2, 2 * BLOCK, 2 * BLOCK)
    arrive_passed(2)
    with jax.named_scope("g_add"):
        add_genes(3, 2 * BLOCK, BLOCK)
    arrive_passed(3)
    with jax.named_scope("g_add"):
        add_genes(3, 3 * BLOCK, BLOCK)
    with jax.named_scope("g_wait_pair"):
        pair_copy.wait_recv()

    with jax.named_scope("h_solve1"):
        counted = pair_own[...] + pair_in[...]
        gradient = counted - total[packed : packed + width] - RIDGE * old
        found = old + solve_packed(
            lambda start, rows: total[start : start + rows], gradient, width, lower_ref
        )
        all_factors[cell, :, mine] = found

    def factors_copy(step):
        place = all_factors.at[cell, :, mine]
        return send(place, place, out_factors, factors_in.at[step // 2], peer(step))

    def factors_relay(step):
        place = all_factors.at[near(step), :, mine]
        return send(place, place, out_relay, relay_in.at[step // 2 - 1], peer(1))

    def factors_relayed(step):
        place = all_factors.at[near(step + 1), :, mine]
        return send(place, place, out_relay, relay_in.at[step // 2 - 1], peer(1))

    def factors_pass(step, place):
        place = all_factors.at[near(step), :, place]
        return send(place, place, out_turn, passed_in.at[step - 1], partner)

    place = all_factors.at[cell, :, mine]
    own_pass = send(place, place, out_own, in_own, partner)
    for step in far + [1]:
        factors_copy(step).start()
    own_pass.start()

    def sum_cells(index, where=slice(None)):
        offsets = jnp.log(all_totals[index, :, where].astype(F32)) - math.log(SCALE_TOTAL)
        rows = all_factors[index, :, where]
        return accumulate(second_left, rows, rows_of(split3(offsets * LOG2E), rows.shape[1]))

    def add_cells(index, where=slice(None)):
        part, extra = sum_cells(index, where)
        sums[...] += part
        sums[packed:] += extra

    with jax.named_scope("k_own1"):
        part, extra = sum_cells(cell, mine)
        sums[...] = part
        sums[packed:] += extra

    with jax.named_scope("i_wait"):
        own_pass.wait_recv()
    with jax.named_scope("i_second"):
        first, second, _ = split3(all_factors[cell])
        stack = jnp.concatenate([first, second, rows_of(split3(offset), cells)], axis=0)
        part = jnp.dot(stack, counts_low[...], preferred_element_type=F32)
        second_own[...] = part[:width]
        whole = loads[0] * (part[:width] + part[width : 2 * width])
        known = jnp.sum(whole, axis=0, keepdims=True)
        for row in range(3):
            known = known + part[2 * width + row : 2 * width + row + 1]
        deviance_own[...] = 2.0 * (constant_part[...] - known)

    for step in steps:
        where = lanes(near(step))
        send(second_own.at[:, where], second_in.at[step - 1], out_second, in_second, peer(step)).start()
        send(deviance_own.at[:, where], deviance_in.at[step - 1], out_deviance, in_deviance, peer(step)).start()

    with jax.named_scope("k_own2"):
        add_cells(cell, theirs)
        new_factors_ref[...] = all_factors[cell]
        take_all(all_totals.at[pl.ds(0, n_cell - 1)], in_totals)

    def take(step):
        if step == 1 or step % 2 == 0:
            factors_copy(step).wait_recv()
            if step > 1:
                factors_relay(step).start()
        else:
            factors_relayed(step - 1).wait_recv()
        factors_pass(step, mine).start()

    order = [2, 1] + far[::-1][1:] + [step + 1 for step in far[::-1]]
    with jax.named_scope("l_wait0"):
        take(order[0])
    for index, step in enumerate(order):
        if index + 1 < len(order):
            with jax.named_scope("l_wait1"):
                take(order[index + 1])
        with jax.named_scope("l_wait2"):
            factors_pass(step, theirs).wait_recv()
        with jax.named_scope("l_add"):
            add_cells(near(step))

    with jax.named_scope("m_wait"):
        take_all(second_in, in_second)
        take_all(deviance_in, in_deviance)

    with jax.named_scope("n_solve2"):
        counted = second_own[:, lanes(cell)]
        deviance = deviance_own[:, lanes(cell)]
        for step in steps:
            counted = counted + second_in[step - 1]
            deviance = deviance + deviance_in[step - 1]
        gradient = counted - sums[packed : packed + width] - RIDGE * own_rows
        new_rows = own_rows + solve_packed(
            lambda start, rows: sums[start : start + rows], gradient, width, lower_ref
        )
        plain = sums[packed + width : packed + width + 1]
        new_loadings_ref[:, lanes(cell)] = new_rows
        deviance_ref[:, lanes(cell)] = (deviance + 2.0 * plain) / (cells * n_cell)

    for step in steps:
        place = new_loadings_ref.at[:, lanes(cell)]
        send(place, place, out_last, in_last, peer(step)).start()
        place = deviance_ref.at[:, lanes(cell)]
        send(place, place, out_tail, in_tail, peer(step)).start()
    with jax.named_scope("o_sends"):
        to_partner.wait_send()
        first_copy.wait_send()
        pair_copy.wait_send()
        own_pass.wait_send()
        take_all(all_totals.at[pl.ds(0, n_cell - 1)], out_totals)
        take_all(loads.at[0], out_across)
        take_all(loads.at[0], out_passed)
        take_all(second_in.at[pl.ds(0, len(far) + 1)], out_factors)
        take_all(second_in.at[pl.ds(0, len(far))], out_relay)
        take_all(second_in, out_turn)
        take_all(second_in, out_second)
        take_all(deviance_in, out_deviance)
    with jax.named_scope("p_last"):
        take_all(second_in, out_last)
        take_all(deviance_in, out_tail)
        take_all(second_in, in_last)
        take_all(deviance_in, in_tail)


def finish_kernel(*refs):
    count = len(refs) // 2
    sem = refs[-1]
    copies = [pltpu.make_async_copy(refs[i], refs[count + i], sem.at[i]) for i in range(count)]
    for copy in copies:
        copy.start()
    for copy in copies:
        copy.wait()


def by_kernel(n_cell, n_gene, counts, totals, cell_factors, gene_loadings):
    cells, genes = counts.shape
    width = cell_factors.shape[1]
    rows = packed_rows(width) + width + 2 * SUB
    chunks = genes // BLOCK
    vmem = pl.BlockSpec(memory_space=pltpu.VMEM)
    hbm = pl.BlockSpec(memory_space=pltpu.HBM)
    dma = lambda *n: pltpu.SemaphoreType.DMA(n)
    shapes = (
        jax.ShapeDtypeStruct((width, cells), F32),
        jax.ShapeDtypeStruct((width, genes), F32),
        jax.ShapeDtypeStruct((1, genes), F32),
    )
    inputs = (counts, totals.reshape(1, cells), cell_factors.T, gene_loadings.T)
    results = pl.pallas_call(
        functools.partial(sweep_kernel, n_cell, n_gene),
        out_shape=shapes,
        in_specs=[hbm] * 4,
        out_specs=(vmem,) * 3,
        scratch_shapes=[
            pltpu.VMEM((cells, genes), jnp.int32),
            pltpu.VMEM((cells, genes), BF16),
            pltpu.VMEM((n_cell, 1, cells), jnp.int32),
            pltpu.VMEM((width, cells), F32),
            pltpu.VMEM((n_gene, width, genes), F32),
            pltpu.VMEM((width, cells), F32),
            pltpu.VMEM((width, LANES), F32),
            pltpu.VMEM((width, LANES), F32),
            pltpu.VMEM((width, LANES), F32),
            pltpu.VMEM((rows, LANES), F32),
            pltpu.VMEM((n_cell, width, cells), F32),
            pltpu.VMEM((1, genes), F32),
            pltpu.VMEM((width, genes), F32),
            pltpu.VMEM((n_cell - 1, width, LANES), F32),
            pltpu.VMEM((1, genes), F32),
            pltpu.VMEM((n_cell - 1, 1, LANES), F32),
            pltpu.VMEM((rows, LANES), F32),
            pltpu.VMEM((1, width * width, LANES), F32),
            dma(4),
            dma(14),
            dma(8),
            dma(1 + 2 * chunks),
            dma(n_cell // 2),
            dma(n_cell // 2 - 1),
            dma(n_cell - 1),
        ],
        compiler_params=pltpu.CompilerParams(
            collective_id=0, has_side_effects=True, vmem_limit_bytes=24000 * 1024
        ),
    )(*[pltpu.with_memory_space_constraint(x, pltpu.HBM) for x in inputs])
    new_factors, new_loadings, deviance = pl.pallas_call(
        finish_kernel,
        out_shape=shapes,
        in_specs=[vmem] * 3,
        out_specs=(hbm,) * 3,
        scratch_shapes=[dma(3)],
        compiler_params=pltpu.CompilerParams(vmem_limit_bytes=8000 * 1024),
    )(*results)
    return (new_factors.T, new_loadings.T, deviance.reshape(genes))


def solution(mesh):
    n_cell, n_gene = mesh.shape["cell"], mesh.shape["gene"]

    def on_device(counts, totals, cell_factors, gene_loadings):
        cells, genes = counts.shape
        whole_lanes = genes == n_cell * LANES and cells == 2 * LANES and genes % BLOCK == 0
        if whole_lanes and n_gene == 4 and n_cell & (n_cell - 1) == 0:
            return by_kernel(n_cell, n_gene, counts, totals, cell_factors, gene_loadings)
        return by_collectives(counts, totals, cell_factors, gene_loadings)

    return jax.shard_map(
        on_device,
        mesh=mesh,
        in_specs=(P("cell", "gene"), P("cell"), P("cell", None), P("gene", None)),
        out_specs=(P("cell", None), P("gene", None), P("gene")),
        check_vma=False,
    )
```

time: 37.4 us -> 30.6 us (0.82)
  local copies, waits for them, and re-layouts: 3.56 us -> 0 us
  Pallas kernels: 33 us -> 29.8 us
    unnamed x8 -> x0, local copies, waits for them, and re-layouts: 3.56 us -> none
    pallas_call x1, Pallas kernels: 32.3 us -> 29.1 us  [by_kernel(): pl.pallas_call(functools.partial(sweep_kernel, n_cell, n_gene), out_shape...]
where the time goes in v1:
time: 30.6 us; the launch traced here: 30.4 us
  Pallas kernels  29.8 us (97%)
  between operations  0.64 us (2%)
    pallas_call x1, Pallas kernels, by_kernel(): pl.pallas_call(functools.partial(sweep_kernel, n_cell, n_gene), out_shape...  29.1 us
    pallas_call x1, Pallas kernels, by_kernel(): pl.pallas_call(finish_kernel, out_shape=shapes, in_specs=[vmem] * 3, out_...  0.7 us

profile of v1, /device:TPU:0, one launch (start us, length us, event | category | flops | bytes accessed | tf_op | source)
XLA Modules:
  0.0 30.4 jit_solution(11615005917556005620)
XLA Ops:
  0.6 29.1 %shard_map.67 = (f32[32,256]{1,0:T(8,128)S(1)}, f32[32,1024]{1,0:T(8,128)S(1)}, f32[1,1024]{1,0:T(1,128)S(1)}) custom-call(s32[256,1024]{1,0:T(8,128)} %counts_hbm.1, s32[1,256]{1,0:T(1,128)} %bitcast.8, f32[32,256]{1,0:T(8,128)} %bitcast.7, f32[32,1024]{1,0:T(8,128)} %bitcast.6), custom_call_target="tpu_custom_call" | custom-call | tf_op jit(solution)/shard_map/pallas_call | solution.py:561
  29.7 0.7 %shard_map.68 = (f32[32,256]{1,0:T(8,128)}, f32[32,1024]{1,0:T(8,128)}, f32[1,1024]{1,0:T(1,128)}) custom-call(f32[32,256]{1,0:T(8,128)S(1)} %get-tuple-element.9.refs_0_, f32[32,1024]{1,0:T(8,128)S(1)} %get-tuple-element.10.refs_1_, f32[1,1024]{1,0:T(1,128)S(1)} %get-tuple-element.11.refs_2_), custom_call_target="tpu_custom_call" | custom-call | tf_op jit(solution)/shard_map/pallas_call | solution.py:597
